TPU v7x, 32 devices: a whole 2x2x4 slice. The times are simulated.
32 devices in a mesh: dp: 8 (over z, x), vocab: 4 (over y, core).
Axes of the slice: x: 2, y: 2, z: 4, core: 2. Of those that a mesh axis runs over, the one named last changes fastest.
Arguments:
- hidden_states: bfloat16 [1024, 3584], P('dp'), may hold values from -40 to 40
- head_weight: bfloat16 [3584, 98304], P(None, ('dp', 'vocab')), as said below
- target_ids: int32 [1024], replicated, may hold values from 0 to 98303
- seq_lengths: int32 [64], P('dp'), may hold values from 1 to 16
- domain_labels: int32 [64], P('dp'), may hold values from 0 to 21
- domain_weights: float32 [22], replicated, may hold values from 0.5 to 4
Outputs:
- token_loss: float32 [1024], P('dp')
- new_weights: float32 [22], replicated
Inputs may be any that keep to these rules, and one draw needn't show every extreme that they name: `head_weight`: every entry lies within 6 / sqrt(3584) of zero.
All inputs are finite; a program needn't handle non-finite values.
Results may differ from a plain program's by a relative error of at most 0.0003.
Values may be sent and summed in bfloat16 or wider, within the bound.
A program may use at most 128 MiB of HBM per device.

v0:
```python
import jax
import jax.numpy as jnp
from jax import lax
from jax.sharding import PartitionSpec as P

SEQ_LEN = 16
DOMAINS = 22


explore_share = 0.01
step_rate = 0.002


def row_statistics(logits, targets, col_start):
    row_peak = jnp.max(logits, axis=1)
    mass_sum = jnp.sum(jnp.exp(logits - row_peak[:, None]), axis=1)
    columns = lax.broadcasted_iota(jnp.int32, logits.shape, 1) + col_start
    picked = jnp.sum(jnp.where(columns == targets[:, None], logits, 0.0), axis=1)
    return (row_peak, mass_sum, picked)


def body(hidden_states, head_weight, target_ids, seq_lengths, domain_labels, domain_weights):
    tok_dev = hidden_states.shape[0]
    col_count = head_weight.shape[1]
    vocab_count = lax.axis_size("vocab")
    dp_count = lax.axis_size("dp")
    dp_index = lax.axis_index("dp")
    vocab_index = lax.axis_index("vocab")
    col_start = (dp_index * vocab_count + vocab_index) * col_count
    own_first = dp_index * tok_dev
    slice_width = hidden_states.shape[1] // vocab_count
    own_part = lax.dynamic_slice_in_dim(hidden_states, vocab_index * slice_width, slice_width, 1)
    tall_part = lax.all_gather(own_part, "dp", axis=0, tiled=True)
    logits = jnp.dot(
        lax.all_gather(tall_part, "vocab", axis=1, tiled=True),
        head_weight,
        preferred_element_type=jnp.float32,
    )
    row_peak, mass_sum, picked = row_statistics(logits, target_ids, col_start)
    global_peak = lax.pmax(row_peak, ("dp", "vocab"))
    scaled = mass_sum * jnp.exp(row_peak - global_peak)
    part_mass, part_pick = (
        lax.psum_scatter(scaled, "dp", scatter_dimension=0, tiled=True),
        lax.psum_scatter(picked, "dp", scatter_dimension=0, tiled=True),
    )
    own_mass, own_pick = lax.psum((part_mass, part_pick), "vocab")
    own_peak = lax.dynamic_slice_in_dim(global_peak, own_first, tok_dev)
    seq_count = seq_lengths.shape[0]
    positions = jnp.arange(tok_dev) % SEQ_LEN
    valid = positions < jnp.repeat(seq_lengths, SEQ_LEN)
    token_loss = jnp.where(valid, jnp.log(own_mass) + own_peak - own_pick, 0.0)
    seq_loss = jnp.sum(token_loss.reshape(seq_count, SEQ_LEN), axis=1)
    seq_tokens = seq_lengths.astype(jnp.float32)
    owned_count = (DOMAINS + dp_count - 1) // dp_count
    padded_count = owned_count * dp_count
    domain_hot = (domain_labels[:, None] == jnp.arange(padded_count)[None, :]).astype(jnp.float32)
    by_owner = jnp.transpose(domain_hot.reshape(seq_count, dp_count, owned_count), (1, 0, 2))
    outgoing = jnp.concatenate(
        [by_owner * seq_loss[None, :, None], by_owner * seq_tokens[None, :, None]], axis=2
    )
    incoming = lax.all_to_all(outgoing, "dp", split_axis=0, concat_axis=0, tiled=True)
    received = jnp.sum(incoming, axis=(0, 1))
    own_loss = received[:owned_count]
    own_count = received[owned_count:]
    first_slot = dp_index * owned_count
    padded_weights = jnp.concatenate(
        [domain_weights, jnp.zeros((padded_count - DOMAINS,), jnp.float32)]
    )
    own_weights = lax.dynamic_slice_in_dim(padded_weights, first_slot, owned_count)
    probability = (1.0 - DOMAINS * explore_share) * own_weights / jnp.sum(
        domain_weights
    ) + explore_share
    reward = own_loss / jnp.maximum(own_count, 1.0) / probability
    raised = own_weights * jnp.exp(step_rate * reward)
    every_raised = lax.all_gather(raised, "dp", axis=0, tiled=True)[:DOMAINS]
    new_weights = DOMAINS * every_raised / jnp.sum(every_raised)
    return (token_loss, new_weights)


def solution(mesh):
    placed = (P("dp", None), P(None, ("dp", "vocab")), P(), P("dp"), P("dp"), P())
    return jax.shard_map(
        body, mesh=mesh, in_specs=placed, out_specs=(P("dp"), P()), check_vma=False
    )
```

profile of v0, /device:TPU:0, one launch (start us, length us, event | category | flops | bytes accessed | tf_op | source)
XLA Modules:
  0.0 253.9 jit_solution(17247480090357435635)
XLA Ops:
  7.2 1.1 copy-done
  8.3 0.7 constant_dynamic-slice_fusion
  9.1 50.2 %all-gather.3.cloned.1.call-done = bf16[1024,896]{1,0:T(8,128)(2,1)} async-done(((bf16[128,896]{1,0:T(8,128)(2,1)}), bf16[1024,896]{1,0:T(8,128)(2,1)}) %all-gather.3.cloned.1.call-update) | async-done | bytes 1835024 | tf_op jit(solution)/shard_map/all_gather | solution.py:33
  59.3 0.7 convert_element_type.6
  60.0 0.7 broadcast_in_dim.10
  60.7 0.1 reshape.30
  60.8 1.3 fusion
  62.8 49.1 %all-gather.5.cloned.1.call-done = bf16[1024,3584]{1,0:T(8,128)(2,1)} async-done(((bf16[1024,896]{1,0:T(8,128)(2,1)}), bf16[1024,3584]{1,0:T(8,128)(2,1)}) %all-gather.5.cloned.1.call-update) | async-done | bytes 7340048 | tf_op jit(solution)/shard_map/all_gather | solution.py:35
  111.9 30.4 %fusion.1 = (f32[1024]{0:T(1024)S(1)}, f32[1024,3072]{1,0:T(8,128)}) fusion(bf16[1024,3584]{1,0:T(8,128)(2,1)} %all-gather.5.cloned.1.call-done, bf16[3584,3072]{1,0:T(8,128)(2,1)} %param.7), kind=kOutput, calls=%fused_computation.16 | convolution fusion | flops 22551724032 | bytes 41947136 | tf_op jit(solution)/shard_map/dot_general | solution.py:34
  142.3 39.3 %pmax.7 = f32[1024]{0:T(1024)S(1)} all-reduce(f32[1024]{0:T(1024)S(1)} %get-tuple-element.12), channel_id=1, replica_groups=mesh['dp'=8,'vocab'=4] {'dp','vocab'}, use_global_device_ids=true, to_apply=%region_2.3 | all-reduce | flops 1024 | bytes 8192 | tf_op jit(solution)/shard_map/pmax | solution.py:40
  181.6 6.8 %exponential_reduce_fusion = (f32[1024]{0:T(1024)S(1)}, f32[1024]{0:T(1024)S(1)}) fusion(f32[1024,3072]{1,0:T(8,128)} %get-tuple-element.13, f32[1024]{0:T(1024)S(1)} %get-tuple-element.12, s32[1024]{0:T(1024)S(1)} %copy-done.1, s32[3072]{0:T(1024)S(1)} %iota_add_fusion), kind=kLoop, calls=%fused_computation.1 | loop fusion | flops 15726592 | bytes 12611584 | tf_op jit(solution)/shard_map/reduce_sum | solution.py:16
  188.3 21.3 %all-reduce.4 = (f32[1024]{0:T(1024)S(1)}, f32[1024]{0:T(1024)S(1)}) all-reduce(f32[1024]{0:T(1024)S(1)} %get-tuple-element.3, f32[1024]{0:T(1024)S(1)} %exponential_multiply_fusion), channel_id=3, replica_groups=mesh['dp'=8,'vocab'=4] {'dp'}, use_global_device_ids=true, to_apply=%region_6.7.clone | all-reduce | flops 2048 | bytes 16384
  209.8 5.6 %all-reduce.5 = (f32[128]{0:T(128)S(1)}, f32[128]{0:T(128)S(1)}) all-reduce(f32[128]{0:T(128)S(1)} %dynamic-slice.4, f32[128]{0:T(128)S(1)} %dynamic-slice.2), channel_id=1, replica_groups=mesh['dp'=8,'vocab'=4] {'vocab'}, use_global_device_ids=true, to_apply=%region_7.8 | all-reduce | flops 256 | bytes 2048 | tf_op jit(solution)/shard_map/psum | solution.py:46
  215.5 0.1 compare_select_fusion.2
  215.6 0.1 reduce_sum.56
  215.8 0.6 pad_maximum_fusion
  216.4 3.3 %all-to-all-start = ((f32[8,8,6]{1,2,0:T(8,128)}), f32[8,8,6]{1,2,0:T(8,128)S(1)}, u32[]{:S(2)}, u32[]{:S(2)}) async-start(f32[8,8,6]{1,2,0:T(8,128)} %pad_maximum_fusion), calls=%async_computation | async-start | bytes 65536 | tf_op jit(solution)/shard_map/all_to_all | solution.py:61
  219.8 0.6 reduce_sum.58
  221.1 5.3 %all-to-all-done = f32[8,8,6]{1,2,0:T(8,128)S(1)} async-done(((f32[8,8,6]{1,2,0:T(8,128)}), f32[8,8,6]{1,2,0:T(8,128)S(1)}, u32[]{:S(2)}, u32[]{:S(2)}) %all-to-all-start) | async-done | bytes 1568 | tf_op jit(solution)/shard_map/all_to_all | solution.py:61
  226.4 0.1 reduce_sum.57
  226.5 0.8 multiply_dynamic-update-slice_fusion
  227.4 17.8 %all-reduce.1 = f32[24]{0:T(128)S(1)} all-reduce(f32[24]{0:T(128)S(1)} %multiply_dynamic-update-slice_fusion), channel_id=1, replica_groups=mesh['dp'=8,'vocab'=4] {'dp'}, use_global_device_ids=true, to_apply=%add.1 | all-reduce | flops 24 | bytes 192
  245.1 0.7 slice_reduce_fusion
  245.8 1.2 multiply_divide_fusion
  (21 shorter events, 0.5 us)
Async XLA Ops:
  7.2 1.2 copy-start
  7.2 52.1 %all-gather.3.cloned.1.call-start = ((), (), s32[]{:S(2)}) async-start(), calls=%async_computation.1 | async-start | bytes 2064384 | tf_op jit(solution)/shard_map/all_gather | solution.py:33
  9.1 102.8 %all-gather.5.cloned.1.call-start = ((), (), s32[]{:S(2)}) async-start(), calls=%async_computation.2 | async-start | bytes 9175040 | tf_op jit(solution)/shard_map/all_gather | solution.py:35
  62.8 118.8 %copy-start.1 = (s32[1024]{0:T(1024)S(1)}, s32[1024]{0:T(1024)}, u32[]{:S(2)}) copy-start(s32[1024]{0:T(1024)} %param.8) | copy-start | bytes 12292
  142.3 73.4 %copy-start.3 = (s32[8]{0:T(128)S(1)}, s32[8]{0:T(128)}, u32[]{:S(2)}) copy-start(s32[8]{0:T(128)} %param.10) | copy-start | bytes 100
  142.3 77.5 %copy-start.4 = (f32[22]{0:T(128)S(1)}, f32[22]{0:T(128)}, u32[]{:S(2)}) copy-start(f32[22]{0:T(128)} %param.11) | copy-start | bytes 268
  215.5 31.5 %copy-start.2 = (f32[128]{0:T(128)}, f32[128]{0:T(128)S(1)}, u32[]{:S(2)}) copy-start(f32[128]{0:T(128)S(1)} %compare_select_fusion.2) | copy-start | bytes 1540
  216.4 10.0 %all-to-all-start = ((f32[8,8,6]{1,2,0:T(8,128)}), f32[8,8,6]{1,2,0:T(8,128)S(1)}, u32[]{:S(2)}, u32[]{:S(2)}) async-start(f32[8,8,6]{1,2,0:T(8,128)} %pad_maximum_fusion), calls=%async_computation | async-start | bytes 65536 | tf_op jit(solution)/shard_map/all_to_all | solution.py:61
Sparse Core Ops, SparseCore 0:
  10.2 49.0 all-gather.2
  60.9 51.0 all-gather.4
where the time goes:
time: 254 us
  waiting for transfers between devices  105 us (41%)
  blocking collectives  84 us (33%)
  matrix products  30.4 us (12%)
  between operations  15.4 us (6%)
  other arithmetic  11.8 us (5%)
  local copies, waits for them, and re-layouts  4.21 us (2%)
  starting transfers between devices  3.41 us (1%)
    all_gather x1, waiting for transfers between devices, body(): tall_part = lax.all_gather(own_part, 'dp', axis=0, tiled=True)  50.2 us
    all_gather x1, waiting for transfers between devices, body(): lax.all_gather(tall_part, 'vocab', axis=1, tiled=True)  49.1 us
    pmax x1, blocking collectives, body(): global_peak = lax.pmax(row_peak, ('dp', 'vocab'))  39.3 us
    unnamed x2, blocking collectives  39.1 us
    dot_general x1, matrix products, body(): jnp.dot(lax.all_gather(tall_part, 'vocab', axis=1, tiled=True), head_weig...  30.4 us
    reduce_sum x1, other arithmetic, row_statistics(): mass_sum = jnp.sum(jnp.exp(logits - row_peak[:, None]), axis=1)  6.75 us
    psum x1, blocking collectives, body(): own_mass, own_pick = lax.psum((part_mass, part_pick), 'vocab')  5.63 us
    all_to_all x1, waiting for transfers between devices, body(): lax.all_to_all(outgoing, 'dp', split_axis=0, concat_axis=0, tiled=True)  5.33 us
  transfers between devices with their start and end apart: 3, of which 3 were waited for; matrix products, arithmetic and copies ran while one was open for 1% of the time, Pallas kernels for 0%

commit v1 on v0

v1 whole, which is shorter than its diff:
```python
import functools
import math

import jax
import jax.numpy as jnp
from jax import lax
from jax.experimental import pallas as pl
from jax.experimental.pallas import tpu as pltpu
from jax.sharding import PartitionSpec as P

SEQ_LEN = 16
DOMAINS = 22
LANES = 128
DOM_PAD = 24
CORES = 2

explore_share = 0.01
step_rate = 0.002


def nearest(p, i, n):
    if n == 2:
        return p if i == 0 else 1 - p
    m = jnp.minimum(p, n - 1 - p)
    k = (i + 1) // 2
    both = jnp.where(i % 2 == 1, p + k, p - k)
    far = i - m
    one = jnp.where(p + p <= n - 1, p + far, p - far)
    return jnp.where(i <= 2 * m, both, one)


def kernel(Z, X, Y, tok, cols, TN,
           hid_ref, w_ref, tgt_ref, len_ref, lab_ref, dw_ref,
           loss_ref, new_ref,
           buf, w_buf, m_ref, s_ref, p_ref, stat_out, stat_in, dom_out, dom_in,
           own_sem, w_sem, recv_sem, send_sem, st_send, st_recv, dm_send, dm_recv):
    nv = Y * CORES
    dp = Z * X
    ndev = dp * nv
    T = cols // TN
    M = X * tok
    pr = tok // nv
    me = lax.axis_index("dp")
    v = lax.axis_index("vocab")
    z, x = me // X, me % X
    y, c = v // CORES, v % CORES

    own_copy = pltpu.make_async_copy(hid_ref, buf.at[pl.ds(me * tok, tok)], own_sem)
    own_copy.start()

    def w_copy(j):
        return pltpu.make_async_copy(
            w_ref.at[:, pl.ds(pl.multiple_of(j * TN, TN), TN)], w_buf.at[j], w_sem.at[j]
        )

    for j in range(T):
        w_copy(j).start()

    def remote(kind, zs, xs, ys, cs, to):
        piece = ((zs * X + xs) * Y + ys) * CORES + cs
        rows = buf.at[pl.ds(pl.multiple_of(piece * pr, pr), pr)]
        return pltpu.make_async_remote_copy(
            src_ref=rows, dst_ref=rows,
            send_sem=send_sem.at[kind, piece], recv_sem=recv_sem.at[piece],
            device_id=to, device_id_type=pl.DeviceIdType.MESH,
        )

    def push(drain, cond, *what):
        def go():
            r = remote(*what)
            if drain:
                r.wait_send()
            else:
                r.start()
        if cond is None:
            go()
        else:
            pl.when(cond)(go)

    def dev(z_, x_, y_, c_):
        return (z_ * X + x_, y_ * CORES + c_)

    def arrive(drain, zs, xs, ys, cs):
        if not drain:
            remote(0, zs, xs, ys, cs, dev(z, x, y, 1 - c)).wait_recv()

    def line(drain, kind, n, pos, src, at, piece):
        up, down = pos + 1 < n, pos > 0
        if src is not None:
            if n == 2:
                return
            up, down = up & (src < pos), down & (src > pos)
        if n == 2:
            push(drain, None, kind, *piece, at(1 - pos))
            return
        push(drain, up, kind, *piece, at(pos + 1))
        push(drain, down, kind + 1, *piece, at(pos - 1))

    def send_z(drain, src, piece):
        line(drain, 1, Z, z, src, lambda q: dev(q, x, y, c), piece)

    def send_x(drain, src, piece):
        line(drain, 3, X, x, src, lambda q: dev(z, q, y, c), piece)

    def send_y(drain, src, piece):
        line(drain, 5, Y, y, src, lambda q: dev(z, x, q, c), piece)

    def send_c(drain, piece):
        push(drain, None, 0, *piece, dev(z, x, y, 1 - c))

    def y_first(i):
        return i == 0 or i == Z - 1

    def begin(drain):
        send_z(drain, None, (z, x, y, c))
        for k in range(Y):
            send_x(drain, None, (z, x, k, c))

    def z_step(drain, i):
        zs = nearest(z, i, Z)
        piece = (zs, x, y, c)
        arrive(drain, *piece)
        send_z(drain, zs, piece)
        send_y(drain, None, piece)
        send_x(drain, None, piece)
        send_c(drain, piece)

    def first_step(drain, i):
        zs = nearest(z, i, Z)
        if y_first(i):
            for t in range(1, Y):
                ys = nearest(y, t, Y)
                piece = (zs, x, ys, c)
                arrive(drain, *piece)
                send_y(drain, ys, piece)
                send_x(drain, None, piece)
                send_c(drain, piece)
        else:
            for t in range(1, X):
                xs = nearest(x, t, X)
                piece = (zs, xs, y, c)
                arrive(drain, *piece)
                send_x(drain, xs, piece)
                send_y(drain, None, piece)
                send_c(drain, piece)

    def second_step(drain, i):
        zs = nearest(z, i, Z)
        if y_first(i):
            for t in range(1, X):
                xs = nearest(x, t, X)
                for s in range(Y):
                    ys = nearest(y, s, Y)
                    piece = (zs, xs, ys, c)
                    arrive(drain, *piece)
                    send_x(drain, xs, piece)
                    send_c(drain, piece)
        else:
            for t in range(1, Y):
                ys = nearest(y, t, Y)
                for s in range(X):
                    xs = nearest(x, s, X)
                    piece = (zs, xs, ys, c)
                    arrive(drain, *piece)
                    send_y(drain, ys, piece)
                    send_c(drain, piece)

    def core_step(drain, i):
        zs = nearest(z, i, Z)
        for t in range(1 if i == 0 else 0, X):
            xs = nearest(x, t, X)
            for ys in range(Y):
                arrive(drain, zs, xs, ys, 1 - c)

    events = []
    for u in range(Z - 1):
        at = lambda twelfth: min(T - 1, twelfth * T // 12)
        if u == 0:
            if Z > 2:
                events.append((0, at(1), z_step, 2))
            events.append((0, at(5), first_step, 1))
            if Z > 3:
                events.append((0, at(8), z_step, 3))
            if Z > 2:
                events.append((0, at(11), first_step, 2))
        else:
            if u + 3 < Z:
                events.append((u, at(2), z_step, u + 3))
            if u + 2 < Z:
                events.append((u, at(3), first_step, u + 2))
        events.append((u, T - 1, second_step, u + 1))
        events.append((u, T - 1, core_step, u + 1))
    tile_events = [e for e in events if e[2] in (z_step, first_step)]
    end_events = [e for e in events if e[2] in (second_step, core_step)]

    own_copy.wait()
    begin(False)
    if Z > 1:
        z_step(False, 1)
    second_step(False, 0)
    core_step(False, 0)

    lane = lax.broadcasted_iota(jnp.int32, (M, LANES), 1)
    col_start = (me * nv + v) * cols

    def plane(u, _):
        zs = z if Z == 1 else nearest(z, u, Z) if Z != 2 else jnp.where(u == 0, z, 1 - z)
        r0 = pl.multiple_of(zs * M, M)
        m_ref[...] = jnp.full((M, LANES), -1e30, jnp.float32)
        s_ref[...] = jnp.zeros((M, LANES), jnp.float32)
        p_ref[...] = jnp.zeros((M, LANES), jnp.float32)

        def tile(j, _):
            for (eu, ej, fn, i) in tile_events:
                pl.when((u == eu) & (j == ej))(functools.partial(fn, False, i))

            @pl.when(u == 0)
            def _():
                w_copy(j).wait()

            logits = jnp.dot(buf[pl.ds(r0, M), :], w_buf[j], preferred_element_type=jnp.float32)
            off = tgt_ref[pl.ds(r0, M), :] - (col_start + j * TN) - lane
            m_old = m_ref[...]
            parts = [logits[:, g * LANES:(g + 1) * LANES] for g in range(TN // LANES)]
            m_new = m_old
            for a in parts:
                m_new = jnp.maximum(m_new, a)
            s = s_ref[...] * jnp.exp(m_old - m_new)
            pk = p_ref[...]
            for g, a in enumerate(parts):
                s = s + jnp.exp(a - m_new)
                pk = pk + jnp.where(off == g * LANES, a, 0.0)
            m_ref[...] = m_new
            s_ref[...] = s
            p_ref[...] = pk
            return 0

        lax.fori_loop(0, T, tile, 0)

        row_m = jnp.max(m_ref[...], axis=1, keepdims=True)
        row_s = jnp.sum(s_ref[...] * jnp.exp(m_ref[...] - row_m), axis=1, keepdims=True)
        row_p = jnp.sum(p_ref[...], axis=1, keepdims=True)
        packed = jnp.where(lane == 0, row_m, jnp.where(lane == 1, row_s, jnp.where(lane == 2, row_p, 0.0)))
        for xs in range(X):
            stat_out[zs * X + xs] = jnp.transpose(packed[xs * tok:(xs + 1) * tok])[:8]
        for xs in range(X):
            d = zs * X + xs

            @pl.when(d == me)
            def _():
                stat_in[me * nv + v] = stat_out[me]

            for k in range(nv):
                @pl.when((d != me) | (v != k))
                def _():
                    pltpu.make_async_remote_copy(
                        src_ref=stat_out.at[d], dst_ref=stat_in.at[me * nv + v],
                        send_sem=st_send, recv_sem=st_recv,
                        device_id=(d, k), device_id_type=pl.DeviceIdType.MESH,
                    ).start()
        for (eu, ej, fn, i) in end_events:
            pl.when(u == eu)(functools.partial(fn, False, i))
        return 0

    lax.fori_loop(0, Z, plane, 0)

    others = stat_in.at[pl.ds(0, ndev - 1)]
    pltpu.make_async_copy(others, others, st_recv).wait()
    ms = stat_in[:, 0, :]
    peak = jnp.max(ms, axis=0, keepdims=True)
    mass = jnp.sum(stat_in[:, 1, :] * jnp.exp(ms - peak), axis=0, keepdims=True)
    pick = jnp.sum(stat_in[:, 2, :], axis=0, keepdims=True)
    position = lax.broadcasted_iota(jnp.int32, (1, tok), 1) % SEQ_LEN
    valid = position < len_ref[...]
    loss = jnp.where(valid, jnp.log(mass) + peak - pick, 0.0)
    loss_ref[...] = loss
    dom = lax.broadcasted_iota(jnp.int32, (DOM_PAD, tok), 0)
    hot = dom == lab_ref[...]
    d_loss = jnp.sum(jnp.where(hot, loss, 0.0), axis=1, keepdims=True)
    d_count = jnp.sum(jnp.where(hot & valid, 1.0, 0.0), axis=1, keepdims=True)
    dlane = lax.broadcasted_iota(jnp.int32, (DOM_PAD, LANES), 1)
    dom_out[...] = jnp.where(dlane == 0, d_loss, jnp.where(dlane == 1, d_count, 0.0))
    dom_in[me] = dom_out[...]
    for k in range(1, dp):
        pltpu.make_async_remote_copy(
            src_ref=dom_out, dst_ref=dom_in.at[me],
            send_sem=dm_send, recv_sem=dm_recv,
            device_id=((me + k) % dp, v), device_id_type=pl.DeviceIdType.MESH,
        ).start()

    begin(True)
    if Z > 1:
        z_step(True, 1)
    second_step(True, 0)
    for (eu, ej, fn, i) in events:
        fn(True, i)
    pltpu.make_async_copy(others, others, st_send).wait()

    rest = dom_in.at[pl.ds(0, dp - 1)]
    pltpu.make_async_copy(rest, rest, dm_recv).wait()
    total = jnp.sum(dom_in[...], axis=0)
    dom_loss = jnp.sum(jnp.where(dlane == 0, total, 0.0), axis=1, keepdims=True)
    dom_count = jnp.sum(jnp.where(dlane == 1, total, 0.0), axis=1, keepdims=True)
    live = lax.broadcasted_iota(jnp.int32, (DOM_PAD, LANES), 0) < DOMAINS
    weights = jnp.where(live, dw_ref[...], 0.0)
    probability = (1.0 - DOMAINS * explore_share) * weights / jnp.sum(
        weights, axis=0, keepdims=True) + explore_share
    reward = dom_loss / jnp.maximum(dom_count, 1.0) / probability
    raised = jnp.where(live, weights * jnp.exp(step_rate * reward), 0.0)
    new_ref[...] = DOMAINS * raised / jnp.sum(raised, axis=0, keepdims=True)
    pltpu.make_async_copy(rest, rest, dm_send).wait()


def body(hidden_states, head_weight, target_ids, seq_lengths, domain_labels, domain_weights):
    tok, width = hidden_states.shape
    cols = head_weight.shape[1]
    dp = lax.axis_size("dp")
    nv = lax.axis_size("vocab")
    X = math.isqrt(dp // 2)
    Z = dp // X
    Y = nv // CORES
    tokens = dp * tok
    TN = 2 * LANES if cols % (2 * LANES) == 0 else LANES
    T = cols // TN
    M = X * tok
    tgt = jnp.broadcast_to(target_ids[:, None], (tokens, LANES))
    lens = jnp.repeat(seq_lengths, SEQ_LEN)[None, :]
    labs = jnp.repeat(domain_labels, SEQ_LEN)[None, :]
    dw = jnp.broadcast_to(
        jnp.concatenate([domain_weights, jnp.ones((DOM_PAD - DOMAINS,), jnp.float32)])[:, None],
        (DOM_PAD, LANES),
    )
    hbm = pl.BlockSpec(memory_space=pl.ANY)
    vmem = pl.BlockSpec(memory_space=pltpu.VMEM)
    f32 = jnp.float32
    dma = pltpu.SemaphoreType.DMA
    loss, new = pl.pallas_call(
        functools.partial(kernel, Z, X, Y, tok, cols, TN),
        out_shape=(jax.ShapeDtypeStruct((1, tok), f32), jax.ShapeDtypeStruct((DOM_PAD, LANES), f32)),
        in_specs=[hbm, hbm, vmem, vmem, vmem, vmem],
        out_specs=(vmem, vmem),
        scratch_shapes=[
            pltpu.VMEM((tokens, width), hidden_states.dtype),
            pltpu.VMEM((T, width, TN), head_weight.dtype),
            pltpu.VMEM((M, LANES), f32),
            pltpu.VMEM((M, LANES), f32),
            pltpu.VMEM((M, LANES), f32),
            pltpu.VMEM((dp, 8, tok), f32),
            pltpu.VMEM((dp * nv, 8, tok), f32),
            pltpu.VMEM((DOM_PAD, LANES), f32),
            pltpu.VMEM((dp, DOM_PAD, LANES), f32),
            dma(()),
            dma((T,)),
            dma((dp * nv,)),
            dma((7, dp * nv)),
            dma(()), dma(()), dma(()), dma(()),
        ],
        compiler_params=pltpu.CompilerParams(has_side_effects=True, vmem_limit_bytes=60 * 2**20),
    )(hidden_states, head_weight, tgt, lens, labs, dw)
    return loss[0], new[:DOMAINS, 0]


def solution(mesh):
    placed = (P("dp", None), P(None, ("dp", "vocab")), P(), P("dp"), P("dp"), P())
    return jax.shard_map(
        body, mesh=mesh, in_specs=placed, out_specs=(P("dp"), P()), check_vma=False
    )
```

time: 254 us -> 106 us (0.42)
  waiting for transfers between devices: 105 us -> 0 us
  Pallas kernels: 0 us -> 97.3 us
  blocking collectives: 84 us -> 0 us
  matrix products: 30.4 us -> 0 us
  between operations: 15.4 us -> 0.64 us
  other arithmetic: 11.8 us -> 0 us
  local copies, waits for them, and re-layouts: 4.21 us -> 8.15 us
  starting transfers between devices: 3.41 us -> 0 us
    all_gather x2 -> x0, waiting for transfers between devices: 99.3 us -> none  [the longest x1 50.2 us: body(): tall_part = lax.all_gather(own_part, 'dp', axis=0, tiled=True)]
    pallas_call x0 -> x1, Pallas kernels: none -> 97.3 us  [body(): pl.pallas_call(functools.partial(kernel, Z, X, Y, tok, cols, TN), out_sha...]
    pmax x1 -> x0, blocking collectives: 39.3 us -> none  [body(): global_peak = lax.pmax(row_peak, ('dp', 'vocab'))]
    unnamed x2 -> x0, blocking collectives: 39.1 us -> none
    dot_general x1 -> x0, matrix products: 30.4 us -> none  [body(): jnp.dot(lax.all_gather(tall_part, 'vocab', axis=1, tiled=True), head_weig...]
    reduce_sum x5 -> x0, other arithmetic: 8.31 us -> none  [the longest x1 6.75 us: row_statistics(): mass_sum = jnp.sum(jnp.exp(logits - row_peak[:, None]), axis=1)]
    psum x1 -> x0, blocking collectives: 5.63 us -> none  [body(): own_mass, own_pick = lax.psum((part_mass, part_pick), 'vocab')]
    all_to_all x1 -> x0, waiting for transfers between devices: 5.33 us -> none  [body(): lax.all_to_all(outgoing, 'dp', split_axis=0, concat_axis=0, tiled=True)]
  transfers between devices with their start and end apart: 3 -> 0, of which waited for: 3 -> 0; matrix products, arithmetic and copies ran while one was open for 1% -> 0% of each run, Pallas kernels for 0% -> 0%
where the time goes in v1:
time: 106 us
  Pallas kernels  97.3 us (92%)
  local copies, waits for them, and re-layouts  8.15 us (8%)
    pallas_call x1, Pallas kernels, body(): pl.pallas_call(functools.partial(kernel, Z, X, Y, tok, cols, TN), out_sha...  97.3 us

profile of v1, /device:TPU:0, one launch (start us, length us, event | category | flops | bytes accessed | tf_op | source)
XLA Modules:
  0.0 106.0 jit_solution(1786035296290540315)
XLA Ops:
  0.6 0.7 concatenate.3
  1.3 0.7 broadcast_in_dim.9
  2.0 0.6 broadcast_in_dim_reshape.6.len_ref
  2.6 0.7 broadcast_in_dim.20
  3.3 0.6 broadcast_in_dim_reshape.7.lab_ref
  3.9 0.7 broadcast_in_dim.21.dw_ref
  4.6 1.7 %broadcast_in_dim.8.tgt_ref = s32[1024,128]{1,0:T(8,128)} broadcast(s32[1024]{0:T(1024)} %param.8), dimensions={0} | broadcast | bytes 528384 | tf_op jit(solution)/shard_map/broadcast_in_dim | solution.py:326
  6.3 97.3 %shard_map.77 = (f32[1,128]{1,0:T(1,128)}, f32[24,128]{1,0:T(8,128)}) custom-call(bf16[128,3584]{1,0:T(8,128)(2,1)} %hid_ref.1, bf16[3584,3072]{1,0:T(8,128)(2,1)} %w_ref.1, s32[1024,128]{1,0:T(8,128)} %broadcast_in_dim.8.tgt_ref, s32[1,128]{1,0:T(1,128)} %broadcast_in_dim_reshape.6.len_ref, s32[1,128]{1,0:T(1,128)} %broadcast_in_dim_reshape.7.lab_ref, ...), custom_call_target="tpu_custom_call" | custom-call | tf_op jit(solution)/shard_map/pallas_call | solution.py:337
  103.5 1.3 %slice_reduce_fusion = f32[22]{0:T(128)} fusion(f32[24,128]{1,0:T(8,128)} %get-tuple-element.5), kind=kLoop, calls=%fused_computation | loop fusion | bytes 176 | tf_op jit(solution)/shard_map/slice | solution.py:360
  104.9 1.2 %copy.9 = f32[128]{0:T(128)} copy(f32[128]{0:T(128)} %bitcast.1) | data formatting | bytes 1024

commit v2 on v1

--- a/solution.py
+++ b/solution.py
@@ -176,13 +176,11 @@
     for u in range(Z - 1):
         at = lambda twelfth: min(T - 1, twelfth * T // 12)
         if u == 0:
+            events.append((0, at(0), first_step, 1))
+            if Z > 3:
+                events.append((0, at(2), z_step, 3))
             if Z > 2:
-                events.append((0, at(1), z_step, 2))
-            events.append((0, at(5), first_step, 1))
-            if Z > 3:
-                events.append((0, at(8), z_step, 3))
-            if Z > 2:
-                events.append((0, at(11), first_step, 2))
+                events.append((0, at(6), first_step, 2))
         else:
             if u + 3 < Z:
                 events.append((u, at(2), z_step, u + 3))
@@ -197,6 +195,8 @@
     begin(False)
     if Z > 1:
         z_step(False, 1)
+    if Z > 2:
+        z_step(False, 2)
     second_step(False, 0)
     core_step(False, 0)
 
@@ -291,6 +291,8 @@
     begin(True)
     if Z > 1:
         z_step(True, 1)
+    if Z > 2:
+        z_step(True, 2)
     second_step(True, 0)
     for (eu, ej, fn, i) in events:
         fn(True, i)

time: 106 us -> 105 us (level)
  Pallas kernels: 97.3 us -> 95.7 us
    pallas_call x1, Pallas kernels: 97.3 us -> 95.7 us  [body(): pl.pallas_call(functools.partial(kernel, Z, X, Y, tok, cols, TN), out_sha...]
where the time goes in v2:
time: 105 us; the launch traced here: 104 us
  Pallas kernels  95.7 us (91%)
  local copies, waits for them, and re-layouts  8.15 us (8%)
    pallas_call x1, Pallas kernels, body(): pl.pallas_call(functools.partial(kernel, Z, X, Y, tok, cols, TN), out_sha...  95.7 us

profile of v2, /device:TPU:0, one launch (start us, length us, event | category | flops | bytes accessed | tf_op | source)
XLA Modules:
  0.0 104.4 jit_solution(15608727120045090219)
XLA Ops:
  0.6 0.7 concatenate.3
  1.3 0.7 broadcast_in_dim.9
  2.0 0.6 broadcast_in_dim_reshape.6.len_ref
  2.6 0.7 broadcast_in_dim.20
  3.3 0.6 broadcast_in_dim_reshape.7.lab_ref
  3.9 0.7 broadcast_in_dim.21.dw_ref
  4.6 1.7 %broadcast_in_dim.8.tgt_ref = s32[1024,128]{1,0:T(8,128)} broadcast(s32[1024]{0:T(1024)} %param.8), dimensions={0} | broadcast | bytes 528384 | tf_op jit(solution)/shard_map/broadcast_in_dim | solution.py:328
  6.3 95.7 %shard_map.77 = (f32[1,128]{1,0:T(1,128)}, f32[24,128]{1,0:T(8,128)}) custom-call(bf16[128,3584]{1,0:T(8,128)(2,1)} %hid_ref.1, bf16[3584,3072]{1,0:T(8,128)(2,1)} %w_ref.1, s32[1024,128]{1,0:T(8,128)} %broadcast_in_dim.8.tgt_ref, s32[1,128]{1,0:T(1,128)} %broadcast_in_dim_reshape.6.len_ref, s32[1,128]{1,0:T(1,128)} %broadcast_in_dim_reshape.7.lab_ref, ...), custom_call_target="tpu_custom_call" | custom-call | tf_op jit(solution)/shard_map/pallas_call | solution.py:339
  101.9 1.3 %slice_reduce_fusion = f32[22]{0:T(128)} fusion(f32[24,128]{1,0:T(8,128)} %get-tuple-element.5), kind=kLoop, calls=%fused_computation | loop fusion | bytes 176 | tf_op jit(solution)/shard_map/slice | solution.py:362
  103.3 1.2 %copy.9 = f32[128]{0:T(128)} copy(f32[128]{0:T(128)} %bitcast.1) | data formatting | bytes 1024
